TPU v7x, 32 devices: a whole 2x2x4 slice. The times are simulated.
32 devices in a mesh: station: 16 (over z, x, core), chan: 2 (over y).
Axes of the slice: x: 2, y: 2, z: 4, core: 2. Of those that a mesh axis runs over, the one named last changes fastest.
Arguments:
- samples: float32 [2, 16, 256, 128, 256], P(None, 'station', 'chan'), may hold values from -6 to 6
- weights: float32 [2, 16, 32, 256, 256], P(None, 'station', None, 'chan'), may hold values from -6 to 6
- antenna_flags: int32 [16, 256], P('station', 'chan'), may hold values from 0 to 1, as said below
- subband_table: int32 [256], replicated, may hold values from 0 to 255, each once
Outputs:
- visibilities: float32 [256, 2, 16, 32, 16], P('chan', None, 'station')
Inputs may be any that keep to these rules, and one draw needn't show every extreme that they name: `antenna_flags`: every station has at least 32 antennas with flag 1. `subband_table`: a permutation of 0 to 255.
All inputs are finite; a program needn't handle non-finite values.
Results may differ from a plain program's by a relative error of at most 0.0019.
Values may be sent and summed in bfloat16 or wider, within the bound.
A program may use at most 192 MiB of HBM per device.

v0:
```python
import jax
import jax.numpy as jnp
from jax import lax
from jax.sharding import PartitionSpec as P


def beamform(steer, signal):

    def contract(left, right):
        return jnp.einsum(
            "sabf,satf->fsbt",
            left,
            right,
            precision=lax.Precision.HIGHEST,
            preferred_element_type=jnp.float32,
        )

    real_part = contract(steer[0], signal[0]) - contract(steer[1], signal[1])
    imag_part = contract(steer[0], signal[1]) + contract(steer[1], signal[0])
    return jnp.stack([real_part, imag_part], axis=1)


def correlate(stacked, arrived):
    return jnp.einsum("ofcsbt,fcrbt->fosbr", stacked, arrived, preferred_element_type=jnp.float32)


def with_swapped(beam_data):
    swapped = jnp.stack([beam_data[:, 1], -beam_data[:, 0]], axis=1)
    return jnp.stack([beam_data, swapped], axis=0)


def on_device(samples, weights, antenna_flags, subband_table):
    usable = antenna_flags.astype(jnp.float32)
    usable_count = lax.psum(jnp.sum(usable, axis=1), "chan")
    gain_scale = lax.rsqrt(usable_count)
    masked = samples * usable[None, :, :, None, None]
    steer = jnp.swapaxes(weights, 2, 3)
    beam_sum = lax.psum_scatter(
        beamform(jnp.take(steer, subband_table, axis=4), jnp.take(masked, subband_table, axis=4)),
        "chan",
        scatter_dimension=0,
        tiled=True,
    )
    beam_data = (beam_sum * gain_scale[None, None, :, None, None]).astype(jnp.bfloat16)
    stacked = with_swapped(beam_data)
    return correlate(stacked, lax.all_gather(beam_data, "station", axis=2, tiled=True))


def solution(mesh):
    in_specs = (
        P(None, "station", "chan", None, None),
        P(None, "station", None, "chan", None),
        P("station", "chan"),
        P(),
    )
    out_specs = P("chan", None, "station", None, None)
    return jax.shard_map(
        on_device, mesh=mesh, in_specs=in_specs, out_specs=out_specs, check_vma=False
    )
```

profile of v0, /device:TPU:0, one launch (start us, length us, event | category | flops | bytes accessed | tf_op | source)
XLA Modules:
  0.0 543.0 jit_solution(18153403711742747376)
XLA Ops:
  6.5 0.7 compare_select_fusion
  7.2 0.7 compare_and_fusion
  7.9 35.5 %copy.45 = f32[2,1,128,128,256]{3,2,0,4,1:T(8,128)} copy(f32[2,1,128,128,256]{4,3,2,1,0:T(8,128)} %param.4) | data formatting | bytes 67108864 | tf_op args[0]
  43.4 10.3 %copy.43 = f32[2,1,32,128,256]{3,2,0,4,1:T(8,128)} copy(f32[2,1,32,128,256]{4,3,2,1,0:T(8,128)} %param.5) | data formatting | bytes 16777216 | tf_op args[1]
  53.8 23.7 %multiply_bitcast_fusion = f32[2,128,128,256]{2,1,0,3:T(8,128)} fusion(f32[2,1,128,128,256]{3,2,0,4,1:T(8,128)} %copy.45, f32[128]{0:T(128)S(1)} %convert_bitcast_fusion), kind=kLoop, calls=%fused_computation.5 | loop fusion | flops 8388608 | bytes 67109376 | tf_op jit(solution)/shard_map/mul | solution.py:36
  77.4 23.6 %gather_fusion.1 = f32[256,2,128,128]{3,2,1,0:T(8,128)} fusion(f32[2,128,128,256]{2,1,0,3:T(8,128)} %multiply_bitcast_fusion, s32[1024]{0:T(1024)S(1)} %pad_clamp_fusion), kind=kCustom, calls=%fused_computation.1 | custom fusion | bytes 67109888 | tf_op jit(solution)/shard_map/jit(_take)/gather | solution.py:39
  101.0 7.7 %gather_fusion = f32[256,2,128,32]{2,3,1,0:T(8,128)} fusion(f32[2,128,32,256]{1,2,0,3:T(8,128)} %bitcast.80, s32[1024]{0:T(1024)S(1)} %pad_clamp_fusion), kind=kCustom, calls=%fused_computation | custom fusion | bytes 16778240 | tf_op jit(solution)/shard_map/jit(_take)/gather | solution.py:39
  108.7 12.9 %bitcast_select_fusion = f32[2,1,128,128,256]{3,2,4,1,0:T(8,128)S(1)} fusion(f32[256,2,128,128]{3,2,1,0:T(8,128)} %gather_fusion.1, pred[256]{0:T(512)(128)(4,1)S(1)} %compare_and_fusion), kind=kLoop, calls=%fused_computation.2 | loop fusion | flops 8388608 | bytes 67109120 | tf_op jit(solution)/shard_map/jit(_take)/select_n | solution.py:39
  121.6 6.0 %bitcast_select_fusion.1 = f32[2,1,128,32,256]{2,3,4,1,0:T(8,128)} fusion(f32[256,2,128,32]{2,3,1,0:T(8,128)} %gather_fusion, pred[256]{0:T(512)(128)(4,1)S(1)} %compare_and_fusion), kind=kLoop, calls=%fused_computation.14 | loop fusion | flops 2097152 | bytes 16777472 | tf_op jit(solution)/shard_map/jit(_take)/select_n | solution.py:39
  127.6 17.8 %fusion.3 = f32[256,32,128]{2,1,0:T(8,128)} fusion(f32[2,1,128,128,256]{3,2,4,1,0:T(8,128)S(1)} %bitcast_select_fusion, f32[2,1,128,32,256]{2,3,4,1,0:T(8,128)} %bitcast_select_fusion.1), kind=kOutput, calls=%fused_computation.9 | convolution fusion | flops 1610612736 | bytes 25165824 | tf_op jit(solution)/shard_map/sabf,satf->fsbt/dot_general | solution.py:10
  145.4 18.0 %fusion.2 = f32[256,32,128]{2,1,0:T(8,128)} fusion(f32[2,1,128,128,256]{3,2,4,1,0:T(8,128)S(1)} %bitcast_select_fusion, f32[2,1,128,32,256]{2,3,4,1,0:T(8,128)} %bitcast_select_fusion.1), kind=kOutput, calls=%fused_computation.8 | convolution fusion | flops 1610612736 | bytes 25165824 | tf_op jit(solution)/shard_map/sabf,satf->fsbt/dot_general | solution.py:10
  163.4 18.7 %subtract_bitcast_fusion = f32[256,1,1,32,128]{4,3,0,2,1:T(8,128)} fusion(f32[256,32,128]{2,1,0:T(8,128)} %fusion.3, f32[2,1,128,128,256]{3,2,4,1,0:T(8,128)S(1)} %bitcast_select_fusion, f32[2,1,128,32,256]{2,3,4,1,0:T(8,128)} %bitcast_select_fusion.1), kind=kOutput, calls=%fused_computation.23 | convolution fusion | flops 1611661312 | bytes 29360128 | tf_op jit(solution)/shard_map/sabf,satf->fsbt/dot_general | solution.py:10
  182.0 19.0 %add_bitcast_fusion = f32[256,1,1,32,128]{4,3,0,2,1:T(8,128)} fusion(f32[256,32,128]{2,1,0:T(8,128)} %fusion.2, f32[2,1,128,128,256]{3,2,4,1,0:T(8,128)S(1)} %bitcast_select_fusion, f32[2,1,128,32,256]{2,3,4,1,0:T(8,128)} %bitcast_select_fusion.1), kind=kOutput, calls=%fused_computation.22 | convolution fusion | flops 1611661312 | bytes 29360128 | tf_op jit(solution)/shard_map/sabf,satf->fsbt/dot_general | solution.py:10
  201.1 4.4 pad_maximum_fusion
  205.5 1.4 copy.53
  207.0 10.9 %copy.65 = f32[32,8,64,128]{3,1,2,0:T(8,128)} copy(f32[32,8,64,128]{3,2,1,0:T(8,128)S(1)} %bitcast.81) | data formatting | bytes 16777216
  217.8 0.0 reduce-scatter.5.cloned.1.call-update
  217.9 0.0 all-gather.2.cloned.1.call-start
  217.9 0.6 convert_reduce_fusion
  218.5 6.7 %psum.7 = f32[1]{0:T(128)} all-reduce(f32[1]{0:T(128)} %bitcast.14), channel_id=1, replica_groups=mesh['station'=16,'chan'=2] {'chan'}, use_global_device_ids=true, to_apply=%region_2.3 | all-reduce | flops 1 | bytes 8 | tf_op jit(solution)/shard_map/psum | solution.py:34
  225.9 94.1 %reduce-scatter.5.cloned.1.call-done = f32[128,8192]{1,0:T(8,128)} async-done(((f32[256,8192]{1,0:T(8,128)}), f32[128,8192]{1,0:T(8,128)}) %reduce-scatter.5.cloned.1.call-update) | async-done | bytes 4194320
  320.1 2.9 copy.57
  323.0 1.9 copy-done
  324.9 1.9 fusion.8
  326.9 1.9 fusion.13
  328.8 0.2 maximum_bitcast_fusion.4
  329.0 6.9 %copy.49 = bf16[1,128,2,1,32,128]{5,0,2,4,1,3:T(2,128)(2,1)} copy(bf16[1,128,2,1,32,128]{5,4,2,1,3,0:T(8,128)(2,1)S(1)} %maximum_bitcast_fusion.4) | data formatting | bytes 4194304 | tf_op jit(solution)/shard_map/stack | solution.py:29
  336.0 0.6 fusion.14
  336.6 6.9 %copy.48 = bf16[1,128,2,1,32,128]{5,0,2,4,1,3:T(2,128)(2,1)} copy(bf16[1,128,2,1,32,128]{5,4,2,1,3,0:T(8,128)(2,1)S(1)} %fusion.14) | data formatting | bytes 4194304 | tf_op jit(solution)/shard_map/stack | solution.py:29
  343.4 151.7 %all-gather.2.cloned.1.call-done = bf16[128,2,16,32,128]{4,3,1,0,2:T(8,128)(2,1)} async-done(((bf16[128,2,1,32,128]{4,3,1,0,2:T(8,128)(2,1)}), bf16[128,2,16,32,128]{4,3,1,0,2:T(8,128)(2,1)}) %all-gather.2.cloned.1.call-update) | async-done | bytes 33554448 | tf_op jit(solution)/shard_map/all_gather | solution.py:46
  495.1 34.7 %fusion.9 = f32[128,2,1,32,16]{4,1,3,0,2:T(2,128)} fusion(bf16[1,128,2,1,32,128]{5,0,2,4,1,3:T(2,128)(2,1)} %copy.49, bf16[1,128,2,1,32,128]{5,0,2,4,1,3:T(2,128)(2,1)} %copy.48, bf16[128,2,16,32,128]{4,3,1,0,2:T(8,128)(2,1)} %all-gather.2.cloned.1.call-done), kind=kOutput, calls=%fused_computation.24 | convolution fusion | flops 75497472 | bytes 38273024 | tf_op jit(solution)/shard_map/ofcsbt,fcrbt->fosbr/dot_general | solution.py:24
  529.8 5.9 %copy.51 = f32[128,2,1,32,16]{0,4,3,2,1:T(8,128)} copy(f32[128,2,1,32,16]{4,1,3,0,2:T(2,128)} %fusion.9) | data formatting | bytes 1048576 | tf_op jit(solution)/shard_map/ofcsbt,fcrbt->fosbr/transpose | solution.py:24
  (9 shorter events, 0.0 us)
Async XLA Ops:
  6.5 313.5 %reduce-scatter.5.cloned.1.call-start = ((), (), s32[]{:S(2)}) async-start(), calls=%async_computation.2 | async-start | bytes 12582912
  7.9 35.5 %copy-start.2 = (s32[1,128]{1,0:T(1,128)S(1)}, s32[1,128]{1,0:T(1,128)}, u32[]{:S(2)}) copy-start(s32[1,128]{1,0:T(1,128)} %param.6) | copy-start | bytes 1540
  217.9 277.2 %all-gather.2.cloned.1.call-start = ((), (), s32[]{:S(2)}) async-start(), calls=%async_computation.1 | async-start | bytes 35651584 | tf_op jit(solution)/shard_map/all_gather | solution.py:46
  323.0 2.0 copy-start
  326.9 9.1 %copy-start.1 = (f32[16,8,64,128]{3,2,1,0:T(8,128)S(1)}, f32[16,8,64,128]{3,2,1,0:T(8,128)}, u32[]{:S(2)}) copy-start(f32[16,8,64,128]{3,2,1,0:T(8,128)} %copy-done) | copy-start | bytes 12582916
Sparse Core Ops, SparseCore 0:
  218.0 102.0 reduce-scatter.4
  327.0 168.0 all-gather.1
where the time goes:
time: 552 us; the launch traced here: 543 us
  waiting for transfers between devices  246 us (45%)
  local copies, waits for them, and re-layouts  114 us (21%)
  matrix products  108 us (20%)
  other arithmetic  53.6 us (10%)
  between operations  14.6 us (3%)
  blocking collectives  6.72 us (1%)
    all_gather x1, waiting for transfers between devices, on_device(): lax.all_gather(beam_data, 'station', axis=2, tiled=True)  152 us
    unnamed x3, waiting for transfers between devices  94.2 us
    dot_general x4, matrix products, contract(): jnp.einsum('sabf,satf->fsbt', left, right, precision=lax.Precision.HIGHES...  73.4 us
    unnamed x11, local copies, waits for them, and re-layouts  63 us
    dot_general x1, matrix products, correlate(): jnp.einsum('ofcsbt,fcrbt->fosbr', stacked, arrived, preferred_element_typ...  34.7 us
    mul x2, other arithmetic, on_device(): masked = samples * usable[None, :, :, None, None]  23.7 us
    gather x1, local copies, waits for them, and re-layouts, on_device(): jnp.take(masked, subband_table, axis=4)  23.6 us
    another operation x2, local copies, waits for them, and re-layouts, with_swapped(): return jnp.stack([beam_data, swapped], axis=0)  13.8 us
  transfers between devices with their start and end apart: 2, of which 2 were waited for; matrix products, arithmetic and copies ran while one was open for 3% of the time, Pallas kernels for 0%

commit v1 on v0

--- a/solution.py
+++ b/solution.py
@@ -43,7 +43,7 @@
     )
     beam_data = (beam_sum * gain_scale[None, None, :, None, None]).astype(jnp.bfloat16)
     stacked = with_swapped(beam_data)
-    return correlate(stacked, lax.all_gather(beam_data, "station", axis=2, tiled=True))
+    return correlate(stacked, jnp.concatenate(lax.all_gather(beam_data, "station"), axis=2))
 
 
 def solution(mesh):

time: 552 us -> 552 us (level)
    all_gather x0 -> x1, local copies, waits for them, and re-layouts: none -> 6.85 us  [on_device(): lax.all_gather(beam_data, 'station')]
    another operation x2 -> x1, local copies, waits for them, and re-layouts: 13.8 us -> 6.94 us  [with_swapped(): return jnp.stack([beam_data, swapped], axis=0)]
where the time goes in v1:
time: 552 us; the launch traced here: 543 us
  waiting for transfers between devices  245 us (44%)
  local copies, waits for them, and re-layouts  114 us (21%)
  matrix products  108 us (20%)
  other arithmetic  54.7 us (10%)
  between operations  14.6 us (3%)
  blocking collectives  6.72 us (1%)
    all_gather x1, waiting for transfers between devices, on_device(): lax.all_gather(beam_data, 'station')  151 us
    unnamed x3, waiting for transfers between devices  94.2 us
    dot_general x4, matrix products, contract(): jnp.einsum('sabf,satf->fsbt', left, right, precision=lax.Precision.HIGHES...  73.4 us
    unnamed x11, local copies, waits for them, and re-layouts  63 us
    dot_general x1, matrix products, correlate(): jnp.einsum('ofcsbt,fcrbt->fosbr', stacked, arrived, preferred_element_typ...  34.7 us
    mul x2, other arithmetic, on_device(): masked = samples * usable[None, :, :, None, None]  23.7 us
    gather x1, local copies, waits for them, and re-layouts, on_device(): jnp.take(masked, subband_table, axis=4)  23.6 us
    select_n x1, other arithmetic, on_device(): jnp.take(masked, subband_table, axis=4)  12.9 us
  transfers between devices with their start and end apart: 2, of which 2 were waited for; matrix products, arithmetic and copies ran while one was open for 3% of the time, Pallas kernels for 0%

profile of v1, /device:TPU:0, one launch (start us, length us, event | category | flops | bytes accessed | tf_op | source)
XLA Modules:
  0.0 543.0 jit_solution(9990091042379952151)
XLA Ops:
  6.5 0.7 compare_select_fusion
  7.2 0.7 compare_and_fusion
  7.9 35.5 %copy.51 = f32[2,1,128,128,256]{3,2,0,4,1:T(8,128)} copy(f32[2,1,128,128,256]{4,3,2,1,0:T(8,128)} %param.4) | data formatting | bytes 67108864 | tf_op args[0]
  43.4 10.3 %copy.49 = f32[2,1,32,128,256]{3,2,0,4,1:T(8,128)} copy(f32[2,1,32,128,256]{4,3,2,1,0:T(8,128)} %param.5) | data formatting | bytes 16777216 | tf_op args[1]
  53.8 23.7 %multiply_bitcast_fusion = f32[2,128,128,256]{2,1,0,3:T(8,128)} fusion(f32[2,1,128,128,256]{3,2,0,4,1:T(8,128)} %copy.51, f32[128]{0:T(128)S(1)} %convert_bitcast_fusion), kind=kLoop, calls=%fused_computation.6 | loop fusion | flops 8388608 | bytes 67109376 | tf_op jit(solution)/shard_map/mul | solution.py:36
  77.4 23.6 %gather_fusion.1 = f32[256,2,128,128]{3,2,1,0:T(8,128)} fusion(f32[2,128,128,256]{2,1,0,3:T(8,128)} %multiply_bitcast_fusion, s32[1024]{0:T(1024)S(1)} %pad_clamp_fusion), kind=kCustom, calls=%fused_computation.1 | custom fusion | bytes 67109888 | tf_op jit(solution)/shard_map/jit(_take)/gather | solution.py:39
  101.0 7.7 %gather_fusion = f32[256,2,128,32]{2,3,1,0:T(8,128)} fusion(f32[2,128,32,256]{1,2,0,3:T(8,128)} %bitcast.93, s32[1024]{0:T(1024)S(1)} %pad_clamp_fusion), kind=kCustom, calls=%fused_computation | custom fusion | bytes 16778240 | tf_op jit(solution)/shard_map/jit(_take)/gather | solution.py:39
  108.7 12.9 %bitcast_select_fusion = f32[2,1,128,128,256]{3,2,4,1,0:T(8,128)S(1)} fusion(f32[256,2,128,128]{3,2,1,0:T(8,128)} %gather_fusion.1, pred[256]{0:T(512)(128)(4,1)S(1)} %compare_and_fusion), kind=kLoop, calls=%fused_computation.4 | loop fusion | flops 8388608 | bytes 67109120 | tf_op jit(solution)/shard_map/jit(_take)/select_n | solution.py:39
  121.6 6.0 %bitcast_select_fusion.1 = f32[2,1,128,32,256]{2,3,4,1,0:T(8,128)} fusion(f32[256,2,128,32]{2,3,1,0:T(8,128)} %gather_fusion, pred[256]{0:T(512)(128)(4,1)S(1)} %compare_and_fusion), kind=kLoop, calls=%fused_computation.15 | loop fusion | flops 2097152 | bytes 16777472 | tf_op jit(solution)/shard_map/jit(_take)/select_n | solution.py:39
  127.6 17.8 %fusion.4 = f32[256,32,128]{2,1,0:T(8,128)} fusion(f32[2,1,128,128,256]{3,2,4,1,0:T(8,128)S(1)} %bitcast_select_fusion, f32[2,1,128,32,256]{2,3,4,1,0:T(8,128)} %bitcast_select_fusion.1), kind=kOutput, calls=%fused_computation.10 | convolution fusion | flops 1610612736 | bytes 25165824 | tf_op jit(solution)/shard_map/sabf,satf->fsbt/dot_general | solution.py:10
  145.4 18.0 %fusion.3 = f32[256,32,128]{2,1,0:T(8,128)} fusion(f32[2,1,128,128,256]{3,2,4,1,0:T(8,128)S(1)} %bitcast_select_fusion, f32[2,1,128,32,256]{2,3,4,1,0:T(8,128)} %bitcast_select_fusion.1), kind=kOutput, calls=%fused_computation.9 | convolution fusion | flops 1610612736 | bytes 25165824 | tf_op jit(solution)/shard_map/sabf,satf->fsbt/dot_general | solution.py:10
  163.4 18.7 %subtract_bitcast_fusion = f32[256,1,1,32,128]{4,3,0,2,1:T(8,128)} fusion(f32[256,32,128]{2,1,0:T(8,128)} %fusion.4, f32[2,1,128,128,256]{3,2,4,1,0:T(8,128)S(1)} %bitcast_select_fusion, f32[2,1,128,32,256]{2,3,4,1,0:T(8,128)} %bitcast_select_fusion.1), kind=kOutput, calls=%fused_computation.24 | convolution fusion | flops 1611661312 | bytes 29360128 | tf_op jit(solution)/shard_map/sabf,satf->fsbt/dot_general | solution.py:10
  182.0 19.0 %add_bitcast_fusion = f32[256,1,1,32,128]{4,3,0,2,1:T(8,128)} fusion(f32[256,32,128]{2,1,0:T(8,128)} %fusion.3, f32[2,1,128,128,256]{3,2,4,1,0:T(8,128)S(1)} %bitcast_select_fusion, f32[2,1,128,32,256]{2,3,4,1,0:T(8,128)} %bitcast_select_fusion.1), kind=kOutput, calls=%fused_computation.23 | convolution fusion | flops 1611661312 | bytes 29360128 | tf_op jit(solution)/shard_map/sabf,satf->fsbt/dot_general | solution.py:10
  201.1 4.4 pad_maximum_fusion
  205.5 1.4 copy.60
  207.0 10.9 %copy.74 = f32[32,8,64,128]{3,1,2,0:T(8,128)} copy(f32[32,8,64,128]{3,2,1,0:T(8,128)S(1)} %bitcast.94) | data formatting | bytes 16777216
  217.9 0.0 all-gather.3.cloned.1.call-start
  217.9 0.6 convert_reduce_fusion
  218.5 6.7 %psum.7 = f32[1]{0:T(128)} all-reduce(f32[1]{0:T(128)} %bitcast.14), channel_id=1, replica_groups=mesh['station'=16,'chan'=2] {'chan'}, use_global_device_ids=true, to_apply=%region_2.3 | all-reduce | flops 1 | bytes 8 | tf_op jit(solution)/shard_map/psum | solution.py:34
  225.9 94.1 %reduce-scatter.5.cloned.1.call-done = f32[128,8192]{1,0:T(8,128)} async-done(((f32[256,8192]{1,0:T(8,128)}), f32[128,8192]{1,0:T(8,128)}) %reduce-scatter.5.cloned.1.call-update) | async-done | bytes 4194320
  320.1 2.9 copy.64
  323.0 1.9 copy-done
  324.9 1.9 fusion.15
  326.9 2.8 fusion.9
  329.7 0.2 fusion.14
  329.9 0.2 maximum_bitcast_fusion.4
  330.1 6.9 %copy.57 = bf16[1,128,2,1,32,128]{5,0,2,4,1,3:T(2,128)(2,1)} copy(bf16[1,128,2,1,32,128]{5,4,2,1,3,0:T(8,128)(2,1)S(1)} %maximum_bitcast_fusion.4) | data formatting | bytes 4194304 | tf_op jit(solution)/shard_map/stack | solution.py:29
  337.1 0.6 fusion.16
  337.7 6.9 %copy.56 = bf16[1,128,2,1,32,128]{5,0,2,4,1,3:T(2,128)(2,1)} copy(bf16[1,128,2,1,32,128]{5,4,2,1,3,0:T(8,128)(2,1)S(1)} %fusion.16) | data formatting | bytes 4194304 | tf_op jit(solution)/shard_map/all_gather | solution.py:46
  344.5 150.6 %all-gather.3.cloned.1.call-done = bf16[2048,2,1,32,128]{4,3,2,1,0:T(8,128)(2,1)} async-done(((bf16[128,2,1,32,128]{4,3,2,1,0:T(8,128)(2,1)}), bf16[2048,2,1,32,128]{4,3,2,1,0:T(8,128)(2,1)}) %all-gather.3.cloned.1.call-update) | async-done | bytes 33554448 | tf_op jit(solution)/shard_map/all_gather | solution.py:46
  495.1 34.7 %fusion.10 = f32[128,2,1,32,16]{4,1,3,0,2:T(2,128)} fusion(bf16[1,128,2,1,32,128]{5,0,2,4,1,3:T(2,128)(2,1)} %copy.57, bf16[1,128,2,1,32,128]{5,0,2,4,1,3:T(2,128)(2,1)} %copy.56, bf16[16,128,2,1,32,128]{5,4,2,1,0,3:T(8,128)(2,1)} %bitcast.96), kind=kOutput, calls=%fused_computation.25 | convolution fusion | flops 75497472 | bytes 38273024 | tf_op jit(solution)/shard_map/ofcsbt,fcrbt->fosbr/dot_general | solution.py:24
  529.8 5.9 %copy.58 = f32[128,2,1,32,16]{0,4,3,2,1:T(8,128)} copy(f32[128,2,1,32,16]{4,1,3,0,2:T(2,128)} %fusion.10) | data formatting | bytes 1048576 | tf_op jit(solution)/shard_map/ofcsbt,fcrbt->fosbr/transpose | solution.py:24
  (10 shorter events, 0.1 us)
Async XLA Ops:
  6.5 313.5 %reduce-scatter.5.cloned.1.call-start = ((), (), s32[]{:S(2)}) async-start(), calls=%async_computation.2 | async-start | bytes 12582912
  7.9 35.5 %copy-start.2 = (s32[1,128]{1,0:T(1,128)S(1)}, s32[1,128]{1,0:T(1,128)}, u32[]{:S(2)}) copy-start(s32[1,128]{1,0:T(1,128)} %param.6) | copy-start | bytes 1540
  217.9 277.2 %all-gather.3.cloned.1.call-start = ((), (), s32[]{:S(2)}) async-start(), calls=%async_computation.1 | async-start | bytes 35651584 | tf_op jit(solution)/shard_map/all_gather | solution.py:46
  323.0 2.0 copy-start
  329.7 7.4 %copy-start.1 = (f32[16,8,64,128]{3,2,1,0:T(8,128)S(1)}, f32[16,8,64,128]{3,2,1,0:T(8,128)}, u32[]{:S(2)}) copy-start(f32[16,8,64,128]{3,2,1,0:T(8,128)} %copy-done) | copy-start | bytes 12582916
Sparse Core Ops, SparseCore 0:
  218.0 102.0 reduce-scatter.4
  327.0 168.0 all-gather.2
